TPU v7x, 32 devices: a whole 2x2x4 slice. The times are simulated.
32 devices in a mesh: ga: 16 (over z, y, x), band: 2 (over core).
Axes of the slice: x: 2, y: 2, z: 4, core: 2. Of those that a mesh axis runs over, the one named last changes fastest.
Arguments:
- coefficients: float32 [2048, 2, 8192], P('band', None, 'ga'), may hold values from -6 to 6
- rotation: float32 [2, 2048, 32], P(None, 'band', 'ga'), may hold values from -0.125 to 0.125
- potential: float32 [64, 4096], P(None, 'ga'), may hold values from -2 to 0.5
- index_map: int32 [8192], replicated, may hold values from 0 to 262143, as said below
- counts: int32 [16], replicated, may hold values from 384 to 512, as said below
Outputs:
- applied_panel: float32 [32, 2, 32, 1024], P(('band', 'ga'))
Inputs may be any that keep to these rules, and one draw needn't show every extreme that they name: counts[i] counts the live slots of index i of ga, which are its slots 0 to counts[i] - 1 of 512; the counts sum to 7168, and some index has exactly 512. `index_map`: live slots name distinct cells, and together exactly 7168 cells whose signed frequency vector has a squared length no larger than that of any cell not named (a ball about the anchor), every signed component of a live cell lying in -16 to 15; dead slots name arbitrary cells.
All inputs are finite; a program needn't handle non-finite values.
Results may differ from a plain program's by a relative error of at most 0.00008.
Values sent between devices are 32-bit elements; how exact they have to be, the bound alone decides.
A program may use at most 128 MiB of HBM per device.

v0:
```python
import functools
import math

import jax
import jax.numpy as jnp
import numpy as np
from jax import lax
from jax.experimental import pallas as pl
from jax.experimental.pallas import tpu as pltpu
from jax.sharding import PartitionSpec as P

F32 = jnp.float32
BF16 = jnp.bfloat16


def split_parts(values):
    high = values.astype(BF16)
    return high, (values - high.astype(F32)).astype(BF16)


def two_parts(table):
    high = table.astype(BF16)
    low = (table - high.astype(np.float32)).astype(BF16)
    return np.stack([high, low])


def tables(box, window, radix):
    half = window // 2
    coarse = window // radix
    k_all = np.arange(box)
    k_coarse = np.arange(box // radix)
    n_signed = np.arange(window) - half
    low = np.arange(radix)
    y_phase = (radix * np.arange(coarse) - half)[:, None] * low[None, :]
    z_phase = n_signed[:, None] * k_all[None, :]
    right = y_phase[:, None, :, None] + z_phase[None, :, None, :]
    right = right.reshape(coarse * window, radix * box) % box
    x_phase = k_all[:, None] * n_signed[None, :]
    l_phase = radix * k_coarse[:, None] * low[None, :]
    left = l_phase[:, None, :, None] + x_phase[None, :, None, :]
    left = left.reshape(k_coarse.size * box, radix * window) % box
    twist = np.repeat(low[:, None] * low[None, :], box, axis=1) % box

    def pair(phase, scale=1.0):
        angle = phase * (2.0 * math.pi / box)
        return (np.stack([np.cos(angle), np.sin(angle)]) * scale).astype(np.float32)

    right_tab = two_parts(pair(right))
    left_pair = pair(left, 1.0 / box**3)
    left_tab = two_parts(left_pair)
    back_tab = two_parts((left_pair * np.float32(box**3)).transpose(0, 2, 1).copy())
    return right_tab, left_tab, back_tab, pair(twist)


def dot3(lhs, rhs, dims=((1,), (0,))):
    def one(a, b):
        return lax.dot_general(a, b, (dims, ((), ())), preferred_element_type=F32)

    return one(lhs[0], rhs[0]) + (one(lhs[0], rhs[1]) + one(lhs[1], rhs[0]))


def block(cos, sin):
    upper = jnp.concatenate([cos, sin], axis=1)
    lower = jnp.concatenate([-sin, cos], axis=1)
    return jnp.concatenate([upper, lower], axis=0)


def whole_kernel(
    bands, groups, box, window, radix, coef_hbm, rot_ref, pot_hbm, row_ref, col_ref,
    right_hbm, left_hbm, back_hbm, twist_ref, out_ref, right_ref, left_ref, back_ref, tab_sem, pot_out, acc, coef, rots, prod, land, vals,
    coef_sem, rot_send, rot_recv, pot_send, pot_recv, pass_send, pass_recv, val_send, val_recv, self_sem
):
    band = lax.axis_index("band")
    me = lax.axis_index("ga")
    total = bands * groups
    flat = band * groups + me
    cols = rot_ref.shape[1] // 2
    own = land.shape[1]
    rows = pot_hbm.shape[0] // bands
    share = pl.ds(pl.multiple_of(band * rows, rows), rows)

    loads = [
        pltpu.make_async_copy(coef_hbm.at[:, c, :], coef.at[c], coef_sem.at[c]) for c in range(2)
    ]
    for load in loads:
        load.start()
    tabs = [
        pltpu.make_async_copy(src, dst, tab_sem.at[i])
        for i, (src, dst) in enumerate(
            ((right_hbm, right_ref), (left_hbm, left_ref), (back_hbm, back_ref))
        )
    ]
    for tab in tabs:
        tab.start()
    rot_self = pltpu.make_async_copy(rot_ref.at[0], rots.at[me], self_sem.at[0])
    rot_self.start()
    pot_self = pltpu.make_async_copy(pot_hbm, pot_out.at[me], self_sem.at[1])
    pot_self.start()

    barrier = pltpu.get_barrier_semaphore()

    def greet(step, carry):
        to = lax.rem(flat + step, total)
        pl.semaphore_signal(
            barrier, inc=1, device_id={"band": to // groups, "ga": lax.rem(to, groups)},
            device_id_type=pl.DeviceIdType.MESH,
        )
        return carry

    lax.fori_loop(1, total, greet, 0)
    pl.semaphore_wait(barrier, total - 1)

    def rot_copy(to, slot):
        return pltpu.make_async_remote_copy(
            src_ref=rot_ref.at[0], dst_ref=rots.at[slot],
            send_sem=rot_send.at[to], recv_sem=rot_recv.at[slot],
            device_id={"band": band, "ga": to}, device_id_type=pl.DeviceIdType.MESH,
        )

    def pot_copy(to, slot):
        return pltpu.make_async_remote_copy(
            src_ref=pot_hbm.at[share], dst_ref=pot_out.at[slot, share],
            send_sem=pot_send.at[to], recv_sem=pot_recv.at[slot],
            device_id={"band": band, "ga": to}, device_id_type=pl.DeviceIdType.MESH,
        )

    def pass_copy(slot, to, holder):
        held = pl.ds(pl.multiple_of(holder * rows, rows), rows)
        return pltpu.make_async_remote_copy(
            src_ref=pot_out.at[slot, held], dst_ref=pot_out.at[slot, held],
            send_sem=pass_send.at[to, slot], recv_sem=pass_recv.at[holder, slot],
            device_id={"band": to, "ga": me}, device_id_type=pl.DeviceIdType.MESH,
        )

    def val_copy(to, slot):
        return pltpu.make_async_remote_copy(
            src_ref=prod.at[pl.ds(to * own, own)], dst_ref=land.at[slot],
            send_sem=val_send.at[to], recv_sem=val_recv.at[slot],
            device_id={"band": to // groups, "ga": lax.rem(to, groups)},
            device_id_type=pl.DeviceIdType.MESH,
        )

    def each(count, mine, act):
        def body(step, carry):
            act(lax.rem(mine + step, count))
            return carry

        lax.fori_loop(1, count, body, 0)

    each(groups, me, lambda to: rot_copy(to, me).start())
    each(groups, me, lambda to: pot_copy(to, me).start())
    for load in loads:
        load.wait()
    rot_self.wait()
    each(groups, me, lambda src: rot_copy(src, src).wait_recv())

    panel = groups * cols
    depth = coef.shape[1]
    real = rots[:, :cols, :].reshape(panel, depth)
    imag = rots[:, cols:, :].reshape(panel, depth)
    high, low = split_parts(jnp.concatenate([real, imag], axis=0))
    both = jnp.concatenate([high, low], axis=0)
    terms = []
    for c in range(2):
        c_high, c_low = split_parts(coef[c])
        first = jnp.dot(both, c_high, preferred_element_type=F32)
        second = jnp.dot(high, c_low, preferred_element_type=F32)
        terms.append(first[: 2 * panel] + (first[2 * panel :] + second))
    prod[:, 0, :] = terms[0][:panel] - terms[1][panel:]
    prod[:, 1, :] = terms[0][panel:] + terms[1][:panel]

    val_self = pltpu.make_async_copy(prod.at[pl.ds(flat * own, own)], land.at[flat], self_sem.at[2])
    val_self.start()
    each(total, flat, lambda to: val_copy(to, flat).start())

    def relay(src):
        pot_copy(src, src).wait_recv()
        each(bands, band, lambda to: pass_copy(src, to, band).start())

    each(groups, me, relay)
    val_self.wait()
    each(total, flat, lambda src: val_copy(src, src).wait_recv())
    summed = land[0:groups]
    for b in range(1, bands):
        summed = summed + land[b * groups : (b + 1) * groups]
    vals[...] = summed
    for tab in tabs:
        tab.wait()

    def pot_ready():
        pot_self.wait()
        each(groups, me, lambda src: each(bands, band, lambda b: pass_copy(src, b, b).wait_recv()))

    for i in range(own):
        apply_kernel(
            box, window, radix, i, pot_ready if i == 0 else None, vals, row_ref, col_ref, pot_out,
            right_ref, left_ref, back_ref, twist_ref, out_ref, acc
        )
    each(total, flat, lambda to: val_copy(to, flat).wait_send())
    each(groups, me, lambda to: rot_copy(to, me).wait_send())
    each(groups, me, lambda to: pot_copy(to, me).wait_send())
    each(groups, me, lambda src: each(bands, band, lambda b: pass_copy(src, b, band).wait_send()))


def run(coefficients, rotation, potential, row_id, col_id, consts, box, window, radix):
    bands, groups = lax.axis_size("band"), lax.axis_size("ga")
    depth, _, slots = coefficients.shape
    cols = rotation.shape[2]
    panel = cols * groups
    own = panel // (bands * groups)
    rot = rotation.transpose(0, 2, 1).reshape(1, 2 * cols, depth)
    hbm = pl.BlockSpec(memory_space=pl.ANY)
    vmem = pl.BlockSpec(memory_space=pltpu.VMEM)
    dma = pltpu.SemaphoreType.DMA
    return pl.pallas_call(
        functools.partial(whole_kernel, bands, groups, box, window, radix),
        out_shape=jax.ShapeDtypeStruct((own, 2, window, window * window), F32),
        in_specs=[hbm, vmem, hbm] + [vmem] * 2 + [hbm] * 3 + [vmem],
        out_specs=vmem,
        scratch_shapes=[
            *[pltpu.VMEM(table.shape, table.dtype) for table in consts[:3]],
            dma((3,)),
            pltpu.VMEM((groups,) + potential.shape, F32),
            pltpu.VMEM((radix * window, 4 * (window // radix) * window), F32),
            pltpu.VMEM((2, depth, slots), F32),
            pltpu.VMEM((groups, 2 * cols, depth), F32),
            pltpu.VMEM((panel, 2, slots), F32),
            pltpu.VMEM((bands * groups, own, 2, slots), F32),
            pltpu.VMEM((groups, own, 2, slots), F32),
            dma((2,)),
            dma((groups,)),
            dma((groups,)),
            dma((groups,)),
            dma((groups,)),
            dma((bands, groups)),
            dma((bands, groups)),
            dma((bands * groups,)),
            dma((bands * groups,)),
            dma((3,)),
        ],
        compiler_params=pltpu.CompilerParams(
            collective_id=0, has_side_effects=True, vmem_limit_bytes=60 * 1024 * 1024
        ),
    )(coefficients, rot, potential, row_id, col_id, *consts)


def apply_kernel(
    box, window, radix, index, pot_ready, val_ref, row_ref, col_ref, pot_ref, right_ref, left_ref, back_ref, twist_ref, out_ref, acc
):
    coarse = window // radix
    rows = radix * window
    cols = coarse * window
    wide = radix * box
    chunk = val_ref.shape[3]
    acc[...] = jnp.zeros_like(acc)

    def scatter(step, carry):
        at = pl.ds(pl.multiple_of(step * chunk, chunk), chunk)
        row_id = row_ref[:, at]
        col_id = col_ref[:, at]
        picks = lax.broadcasted_iota(jnp.int32, (rows, chunk), 0) == row_id
        onehot = jnp.where(picks, 1.0, 0.0).astype(BF16)
        hits = lax.broadcasted_iota(jnp.int32, (cols, chunk), 0) == col_id
        high, low = split_parts(val_ref[step, index])
        high, low = high.astype(F32), low.astype(F32)
        placed = [
            jnp.where(hits, part[c : c + 1, :], 0.0).astype(BF16)
            for part in (high, low)
            for c in range(2)
        ]
        acc[...] += lax.dot_general(
            onehot,
            jnp.concatenate(placed, axis=0),
            (((1,), (1,)), ((), ())),
            preferred_element_type=F32,
        )
        return carry

    lax.fori_loop(0, val_ref.shape[0], scatter, 0)
    grid_field = acc[:, : 2 * cols] + acc[:, 2 * cols :]

    right = [block(right_ref[i, 0], right_ref[i, 1]) for i in range(2)]
    field = dot3(split_parts(grid_field), right)
    cos = twist_ref[0][:, None, :]
    sin = twist_ref[1][:, None, :]
    real = field[:, :wide].reshape(radix, window, wide)
    imag = field[:, wide:].reshape(radix, window, wide)
    turned = jnp.concatenate(
        [
            (real * cos - imag * sin).reshape(rows, wide),
            (real * sin + imag * cos).reshape(rows, wide),
        ],
        axis=0,
    )
    left = [block(left_ref[i, 0], -left_ref[i, 1]) for i in range(2)]
    space = dot3(left, split_parts(turned))
    if pot_ready is not None:
        pot_ready()
    per = pot_ref.shape[0] // (box // radix)
    pot = jnp.concatenate(
        [
            jnp.concatenate([pot_ref[k * per + i] for i in range(per)], axis=1)
            for k in range(box // radix)
        ],
        axis=0,
    )
    space = space * jnp.concatenate([pot, pot], axis=0)
    back = [block(back_ref[i, 0], back_ref[i, 1]) for i in range(2)]
    field = dot3(back, split_parts(space))
    real = field[:rows].reshape(radix, window, wide)
    imag = field[rows:].reshape(radix, window, wide)
    turned = jnp.concatenate(
        [
            (real * cos + imag * sin).reshape(rows, wide),
            (imag * cos - real * sin).reshape(rows, wide),
        ],
        axis=1,
    )
    applied = dot3(split_parts(turned), right, ((1,), (1,)))

    half = window // 2
    row_at = lax.broadcasted_iota(jnp.int32, (rows, cols), 0)
    col_at = lax.broadcasted_iota(jnp.int32, (rows, cols), 1)
    n_x = (row_at % window - half).astype(F32)
    n_y = (col_at // window * radix + row_at // window - half).astype(F32)
    n_z = (col_at % window - half).astype(F32)
    kinetic = (8.0 / (box * box)) * (n_x * n_x + n_y * n_y + n_z * n_z)
    applied = applied + jnp.concatenate([kinetic, kinetic], axis=1) * grid_field
    for c in range(2):
        pieces = [
            applied[lo * window : (lo + 1) * window, c * cols + hi * window : c * cols + (hi + 1) * window]
            for hi in range(coarse)
            for lo in range(radix)
        ]
        out_ref[index, c] = jnp.concatenate(pieces, axis=1)


def per_device(coefficients, rotation, potential, index_map, counts):
    box = potential.shape[0]
    window = box // 2
    half = window // 2
    radix = math.isqrt(box)
    assert radix * radix == box
    slots_each = index_map.shape[0] // counts.shape[0]
    slot_ids = jnp.arange(slots_each, dtype=jnp.int32)
    live = (slot_ids[None, :] < counts[:, None]).reshape(-1)
    cell_x = (index_map // (box * box) + half) % box
    cell_y = (index_map // box % box + half) % box
    cell_z = (index_map % box + half) % box
    inside = (cell_x < window) & (cell_y < window) & (cell_z < window)
    row_id = jnp.where(live & inside, cell_y % radix * window + cell_x, -1)[None]
    col_id = (cell_y // radix * window + cell_z)[None]
    consts = [jnp.asarray(t) for t in tables(box, window, radix)]

    return run(coefficients, rotation, potential, row_id, col_id, consts, box, window, radix)


def solution(mesh):
    placed = (P("band", None, "ga"), P(None, "band", "ga"), P(None, "ga"), P(), P())
    return jax.shard_map(
        per_device,
        mesh=mesh,
        in_specs=placed,
        out_specs=P(("band", "ga"), None, None, None),
        check_vma=False,
    )
```

profile of v0, /device:TPU:0, one launch (start us, length us, event | category | flops | bytes accessed | tf_op | source)
XLA Modules:
  0.0 49.1 jit_solution(9815922233460753711)
XLA Ops:
  0.0 0.7 %fusion.13 = pred[2,4,8,128]{3,2,1,0:T(8,128)(4,1)S(1)} fusion(s32[16]{0:T(128)} %param.13), kind=kLoop, calls=%fused_computation.41 | loop fusion | flops 8192 | bytes 8256
  0.7 1.3 %reshape.8.rot_ref = f32[1,4,1024]{2,1,0:T(4,128)} reshape(f32[2,2,1024]{2,1,0:T(2,128)} %bitcast.9) | data formatting | bytes 32768 | tf_op jit(solution)/shard_map/reshape | solution.py:211
  2.1 1.5 %fusion.12 = (s32[8192]{0:T(1024)}, s32[8192]{0:T(1024)}) fusion(s32[8192]{0:T(1024)} %param.12, pred[8192]{0:T(1024)(128)(4,1)S(1)} %bitcast.8), kind=kLoop, calls=%fused_computation.37 | loop fusion | flops 868352 | bytes 106496 | tf_op jit(solution)/shard_map/add | solution.py:352
  3.6 43.8 %shard_map.91 = f32[1,2,32,1024]{3,2,1,0:T(8,128)} custom-call(f32[1024,2,512]{2,1,0:T(2,128)} %coef_hbm.1, f32[1,4,1024]{2,1,0:T(4,128)} %reshape.8.rot_ref, f32[64,256]{1,0:T(8,128)} %pot_hbm.1, s32[1,8192]{1,0:T(1,128)} %bitcast.7, s32[1,8192]{1,0:T(1,128)} %bitcast.6, bf16[2,2,128,512]{3,2,1,0:T(8,128)(2,1)} %constant.92.clone.right_hbm, ...), custom_call_target="tpu_custom_call" | custom-call | tf_op jit(solution)/shard_map/pallas_call | solution.py:215
  47.4 1.7 %copy.12 = f32[1,2,32,1024]{3,2,1,0:T(8,128)} copy(f32[1,2,32,1024]{3,2,1,0:T(8,128)} %shard_map.91) | data formatting | bytes 524288
  (1 shorter events, 0.0 us)
where the time goes:
time: 49.4 us; the launch traced here: 49.1 us
  Pallas kernels  43.8 us (89%)
  local copies, waits for them, and re-layouts  3.03 us (6%)
  other arithmetic  2.24 us (5%)
    pallas_call x1, Pallas kernels, run(): pl.pallas_call(functools.partial(whole_kernel, bands, groups, box, window...  43.8 us
    unnamed x2, local copies, waits for them, and re-layouts  1.69 us
    add x1, other arithmetic, per_device(): col_id = (cell_y // radix * window + cell_z)[None]  1.52 us
    reshape x1, local copies, waits for them, and re-layouts, run(): rot = rotation.transpose(0, 2, 1).reshape(1, 2 * cols, depth)  1.34 us

commit v1 on v0

v1 whole, which is shorter than its diff:
```python
import functools
import math

import jax
import jax.numpy as jnp
import numpy as np
from jax import lax
from jax.experimental import pallas as pl
from jax.experimental.pallas import tpu as pltpu
from jax.sharding import PartitionSpec as P

F32 = jnp.float32
BF16 = jnp.bfloat16
I32 = jnp.int32
MESH = pl.DeviceIdType.MESH


def split_parts(values):
    high = values.astype(BF16)
    return high, (values - high.astype(F32)).astype(BF16)


def two_parts(table):
    high = table.astype(BF16)
    low = (table - high.astype(np.float32)).astype(BF16)
    return np.stack([high, low])


class Sizes:
    def __init__(self, box, window):
        self.box, self.window, self.half = box, window, window // 2
        self.low = 4
        self.high = window // self.low
        self.span = box // self.low
        self.rows = self.low * window
        self.cols = self.high * window
        self.wide = self.span * box
        self.deep = self.low * box
        self.fold = 2
        self.lanes = self.cols // self.fold
        assert box % self.low == 0 and box == 2 * window and box & (box - 1) == 0


def tables(sz):
    n_signed = np.arange(sz.window) - sz.half
    k_all = np.arange(sz.box)
    y_start = sz.low * np.arange(sz.high) - sz.half
    k_low = np.arange(sz.span)
    digit = np.arange(sz.low)

    def pair(phase):
        angle = (phase % sz.box) * (2.0 * math.pi / sz.box)
        return np.stack([np.cos(angle), np.sin(angle)])

    y_phase = y_start[:, None] * k_low[None, :]
    z_phase = n_signed[:, None] * k_all[None, :]
    base = np.concatenate(
        [pair(np.tile(z_phase, (1, sz.span))), pair(np.repeat(y_phase, sz.box, axis=1))], axis=1
    )
    flip = np.concatenate(
        [pair(np.tile(z_phase.T, (1, sz.high))), pair(np.repeat(y_phase.T, sz.window, axis=1))], axis=1
    )
    twist = pair(np.repeat(digit[:, None] * k_low[None, :], sz.box, axis=1))
    l_phase = sz.span * digit[:, None] * digit[None, :]
    x_phase = k_all[:, None] * n_signed[None, :]
    left = (l_phase[:, None, :, None] + x_phase[None, :, None, :]).reshape(sz.deep, sz.rows)
    cos, sin = pair(left)
    fore = two_parts((np.block([[cos, -sin], [sin, cos]]) / sz.box**3).astype(np.float32))
    back = two_parts(np.block([[cos.T, sin.T], [-sin.T, cos.T]]).astype(np.float32))
    return base.astype(np.float32), flip.astype(np.float32), twist.astype(np.float32), fore, back


def dot(a, b, dims=((1,), (0,))):
    return lax.dot_general(a, b, (dims, ((), ())), preferred_element_type=F32)


def whole_kernel(
    bands, groups, sz, early, coef_hbm, rot_hbm, pot_hbm, idx_hbm, cnt_hbm, base_hbm, flip_hbm, twist_hbm,
    fore_hbm, back_hbm, out_ref, coef, rot_ref, idx, cnt, base, flip, twist, fore, back, right, right_t,
    rows_hot, cols_hot, parts, rots, prod, land, pot, grid, space, kin, load_sem, self_sem, rot_send,
    rot_recv, pot_send, pot_recv, pass_send, pass_recv, val_send, val_recv
):
    band = lax.axis_index("band")
    me = lax.axis_index("ga")
    flat = band * groups + me
    depth, slots = coef.shape[1], coef.shape[2]
    cols = rot_ref.shape[1]
    panel = groups * cols
    own = land.shape[1]
    share_rows = pot_hbm.shape[0] // bands

    def share(holder):
        return pl.ds(pl.multiple_of(holder * share_rows, share_rows), share_rows)

    def load(src, dst, at):
        return pltpu.make_async_copy(src, dst, load_sem.at[at])

    rot_load = load(rot_hbm, rot_ref, 0)
    rot_load.start()
    small = [
        load(src, dst, at + 1)
        for at, (src, dst) in enumerate(
            (
                (base_hbm, base), (flip_hbm, flip), (idx_hbm, idx), (cnt_hbm, cnt), (twist_hbm, twist),
                (fore_hbm, fore), (back_hbm, back),
            )
        )
    ]
    coef_load = [load(coef_hbm.at[:, c, :], coef.at[c], 8 + c) for c in range(2)]
    for item in small[:4] + coef_load + small[4:]:
        item.start()

    barrier = pltpu.get_barrier_semaphore()
    peers = [(db, dg) for db in range(bands) for dg in range(groups) if db or dg]

    def ahead(db, dg):
        return {"band": lax.rem(band + db, bands), "ga": lax.rem(me + dg, groups)}

    def every(act):
        if len(peers) < 64:
            for db, dg in peers:
                act(db, dg)
        else:

            def body(step, carry):
                act(step // groups, lax.rem(step, groups))
                return carry

            lax.fori_loop(1, bands * groups, body, 0)

    def greet(db, dg):
        pl.semaphore_signal(barrier, inc=1, device_id=ahead(db, dg), device_id_type=MESH)

    every(greet)
    rot_load.wait()
    rot_self = pltpu.make_async_copy(rot_hbm, rots.at[me], self_sem.at[0])
    rot_self.start()
    pot_self = pltpu.make_async_copy(pot_hbm.at[share(band)], pot.at[0, share(band)], self_sem.at[1])
    pot_self.start()
    pl.semaphore_wait(barrier, bands * groups - 1)

    def rot_copy(step):
        return pltpu.make_async_remote_copy(
            src_ref=rot_ref, dst_ref=rots.at[me], send_sem=rot_send.at[step], recv_sem=rot_recv.at[step],
            device_id={"band": band, "ga": lax.rem(me + step, groups)}, device_id_type=MESH,
        )

    def pot_copy(step):
        return pltpu.make_async_remote_copy(
            src_ref=pot_hbm.at[share(band)], dst_ref=pot.at[step, share(band)],
            send_sem=pot_send.at[step], recv_sem=pot_recv.at[step],
            device_id={"band": band, "ga": lax.rem(me + step, groups)}, device_id_type=MESH,
        )

    def pass_copy(piece, db, holder):
        held = pot.at[pl.ds(piece[0], piece[1] - piece[0]), share(holder)]
        return pltpu.make_async_remote_copy(
            src_ref=held, dst_ref=held, send_sem=pass_send.at[db, piece[2]], recv_sem=pass_recv.at[db, piece[2]],
            device_id={"band": lax.rem(band + db, bands), "ga": me}, device_id_type=MESH,
        )

    def val_copy(db, dg):
        to = ahead(db, dg)
        return pltpu.make_async_remote_copy(
            src_ref=prod.at[pl.ds((to["band"] * groups + to["ga"]) * own, own)], dst_ref=land.at[db * groups + dg],
            send_sem=val_send.at[db * groups + dg], recv_sem=val_recv.at[db * groups + dg],
            device_id=to, device_id_type=MESH,
        )

    pieces = [(0, early, 0), (early, groups, 1)]
    for step in range(1, groups):
        rot_copy(step).start()
    for step in range(1, early):
        pot_copy(step).start()

    small[0].wait()

    def fill_right(step, carry):
        at = pl.multiple_of(step * sz.window, sz.window)
        y_cos = base[0, pl.ds(sz.window + step, 1), :]
        y_sin = base[1, pl.ds(sz.window + step, 1), :]
        z_cos, z_sin = base[0, : sz.window, :], base[1, : sz.window, :]
        cos = split_parts(z_cos * y_cos - z_sin * y_sin)
        sin = split_parts(z_sin * y_cos + z_cos * y_sin)
        for part in range(2):
            right[part, pl.ds(at, sz.window), : sz.wide] = cos[part]
            right[part, pl.ds(at, sz.window), sz.wide :] = sin[part]
            right[part, pl.ds(sz.cols + at, sz.window), : sz.wide] = -sin[part]
            right[part, pl.ds(sz.cols + at, sz.window), sz.wide :] = cos[part]
        return carry

    lax.fori_loop(0, sz.high, fill_right, 0)
    small[1].wait()

    def fill_right_t(step, carry):
        at = pl.multiple_of(step * sz.box, sz.box)
        y_cos = flip[0, pl.ds(sz.box + step, 1), :]
        y_sin = flip[1, pl.ds(sz.box + step, 1), :]
        z_cos, z_sin = flip[0, : sz.box, :], flip[1, : sz.box, :]
        cos = split_parts(z_cos * y_cos - z_sin * y_sin)
        sin = split_parts(z_sin * y_cos + z_cos * y_sin)
        for part in range(2):
            right_t[part, pl.ds(at, sz.box), : sz.cols] = cos[part]
            right_t[part, pl.ds(at, sz.box), sz.cols :] = -sin[part]
            right_t[part, pl.ds(sz.wide + at, sz.box), : sz.cols] = sin[part]
            right_t[part, pl.ds(sz.wide + at, sz.box), sz.cols :] = cos[part]
        return carry

    lax.fori_loop(0, sz.span, fill_right_t, 0)
    small[2].wait()
    small[3].wait()
    bits = sz.box.bit_length() - 1

    def fill_hot(step, carry):
        at = pl.ds(pl.multiple_of(step * slots, slots), slots)
        cell = idx[:, at]
        n_x = (jnp.right_shift(cell, 2 * bits) + sz.half) & (sz.box - 1)
        n_y = (jnp.right_shift(cell, bits) + sz.half) & (sz.box - 1)
        n_z = (cell + sz.half) & (sz.box - 1)
        live = lax.broadcasted_iota(I32, (1, slots), 1) < cnt[step]
        live = live & (n_x < sz.window) & (n_y < sz.window) & (n_z < sz.window)
        y_high, y_low = n_y // sz.low, n_y % sz.low
        block, fine = y_high // (sz.high // sz.fold), y_high % (sz.high // sz.fold)
        row = jnp.where(live, block * sz.rows + y_low * sz.window + n_x, -1)
        col = fine * sz.window + n_z
        row_at = lax.broadcasted_iota(I32, (sz.fold * sz.rows, slots), 0)
        col_at = lax.broadcasted_iota(I32, (sz.lanes, slots), 0)
        rows_hot[:, at] = jnp.where(row_at == row, 1.0, 0.0).astype(BF16)
        cols_hot[:, at] = jnp.where(col_at == col, 1.0, 0.0).astype(BF16)
        return carry

    lax.fori_loop(0, groups, fill_hot, 0)
    row_at = lax.broadcasted_iota(I32, (sz.rows, sz.cols), 0)
    col_at = lax.broadcasted_iota(I32, (sz.rows, sz.cols), 1)
    n_x = (row_at % sz.window - sz.half).astype(F32)
    n_y = (col_at // sz.window * sz.low + row_at // sz.window - sz.half).astype(F32)
    n_z = (col_at % sz.window - sz.half).astype(F32)
    kin[...] = (8.0 / (sz.box * sz.box)) * (n_x * n_x + n_y * n_y + n_z * n_z)

    slab = 128
    for c in range(2):
        coef_load[c].wait()

        def fill_parts(step, carry, c=c):
            at = pl.multiple_of(step * slab, slab)
            high, low = split_parts(coef[c, pl.ds(at, slab), :])
            parts[0, pl.ds(c * depth + at, slab), :] = high
            parts[1, pl.ds(c * depth + at, slab), :] = low
            return carry

        lax.fori_loop(0, depth // slab, fill_parts, 0)
    for item in small[4:]:
        item.wait()

    rot_self.wait()
    for step in range(1, groups):
        rot_copy(step).wait_recv()
    real = rots[:, 0].reshape(panel, depth)
    imag = rots[:, 1].reshape(panel, depth)
    mixer = jnp.concatenate(
        [jnp.concatenate([real, -imag], axis=1), jnp.concatenate([imag, real], axis=1)], axis=0
    )
    high, low = split_parts(mixer)
    first = dot(jnp.concatenate([high, low], axis=0), parts[0])
    mixed = first[: 2 * panel] + first[2 * panel :] + dot(high, parts[1])
    prod[:, 0, :] = mixed[:panel]
    prod[:, 1, :] = mixed[panel:]

    every(lambda db, dg: val_copy(db, dg).start())
    val_self = prod.at[pl.ds(flat * own, own)]
    for step in range(early, groups):
        pot_copy(step).start()

    def relay(piece):
        for step in range(max(piece[0], 1), piece[1]):
            pot_copy(step).wait_recv()
        for db in range(1, bands):
            pass_copy(piece, db, band).start()

    pot_self.wait()
    relay(pieces[0])

    batch = 4 if groups % 4 == 0 else 1
    for i in range(own):
        for start in range(0, groups, batch):
            total = None
            for dg in range(start, start + batch):
                values = val_self[i] if dg == 0 else None
                for db in range(bands):
                    if i == 0 and (db or dg):
                        val_copy(db, dg).wait_recv()
                    if db or dg:
                        piece = land[db * groups + dg, i]
                        values = piece if values is None else values + piece
                source = lax.rem(me + groups - dg, groups)
                at = pl.ds(pl.multiple_of(source * slots, slots), slots)
                hits = cols_hot[:, at]
                placed = jnp.concatenate(
                    [hits * part[c : c + 1, :] for part in split_parts(values) for c in range(2)], axis=0
                )
                term = dot(rows_hot[:, at], placed, ((1,), (1,)))
                total = term if total is None else total + term
            if start:
                grid[...] += total
            else:
                grid[...] = total
        if i == 0:
            relay(pieces[1])

        def pot_ready():
            for piece in pieces:
                for db in range(1, bands):
                    pass_copy(piece, db, lax.rem(band + bands - db, bands)).wait_recv()

        apply_kernel(
            groups, sz, i, me, pot_ready if i == 0 else None, grid, pot, right, right_t, fore, back, twist, kin, space, out_ref
        )
    every(lambda db, dg: val_copy(db, dg).wait_send())
    for step in range(1, groups):
        rot_copy(step).wait_send()
        pot_copy(step).wait_send()
    for piece in pieces:
        for db in range(1, bands):
            pass_copy(piece, db, band).wait_send()


def apply_kernel(
    groups, sz, index, me, pot_ready, grid, pot, right, right_t, fore, back, twist, kin, space, out_ref
):
    whole = 2 * sz.lanes
    summed = grid[:, :whole] + grid[:, whole:]
    field = jnp.concatenate(
        [
            summed[f * sz.rows : (f + 1) * sz.rows, c * sz.lanes : (c + 1) * sz.lanes]
            for c in range(2)
            for f in range(sz.fold)
        ],
        axis=1,
    )
    field_high, field_low = split_parts(field)
    step = 256
    for at in range(0, sz.wide, step):
        halves = []
        for c in range(2):
            here = slice(c * sz.wide + at, c * sz.wide + at + step)
            halves.append(
                dot(field_high, right[0, :, here])
                + (dot(field_low, right[0, :, here]) + dot(field_high, right[1, :, here]))
            )
        real = halves[0].reshape(sz.low, sz.window, step)
        imag = halves[1].reshape(sz.low, sz.window, step)
        cos = twist[0, :, at : at + step][:, None, :]
        sin = twist[1, :, at : at + step][:, None, :]
        turned = jnp.concatenate(
            [
                (real * cos - imag * sin).reshape(sz.rows, step),
                (real * sin + imag * cos).reshape(sz.rows, step),
            ],
            axis=0,
        )
        high, low = split_parts(turned)
        space[:, at : at + step] = dot(fore[0], high) + (dot(fore[0], low) + dot(fore[1], high))
    if pot_ready is not None:
        pot_ready()
    each = pot.shape[2]
    per = groups // sz.low
    applied = None
    for at in range(0, sz.wide, step):
        blocks = []
        for k_high in range(sz.low):
            lane = []
            for q in range(at // each, (at + step + each - 1) // each):
                lane.append(pot[lax.rem(me + groups - (k_high * per + q), groups)])
            blocks.append(lane[0] if len(lane) == 1 else jnp.concatenate(lane, axis=1))
        local = jnp.concatenate(blocks, axis=0)
        high, low = split_parts(space[:, at : at + step] * jnp.concatenate([local, local], axis=0))
        spread = dot(back[0], high) + (dot(back[0], low) + dot(back[1], high))
        real = spread[: sz.rows].reshape(sz.low, sz.window, step)
        imag = spread[sz.rows :].reshape(sz.low, sz.window, step)
        cos = twist[0, :, at : at + step][:, None, :]
        sin = twist[1, :, at : at + step][:, None, :]
        turned = [
            (real * cos + imag * sin).reshape(sz.rows, step),
            (imag * cos - real * sin).reshape(sz.rows, step),
        ]
        for c in range(2):
            here = slice(c * sz.wide + at, c * sz.wide + at + step)
            high, low = split_parts(turned[c])
            term = dot(high, right_t[0, here, :]) + (
                dot(low, right_t[0, here, :]) + dot(high, right_t[1, here, :])
            )
            applied = term if applied is None else applied + term
    applied = applied + jnp.concatenate([kin[...], kin[...]], axis=1) * field
    for c in range(2):
        pieces = [
            applied[lo * sz.window : (lo + 1) * sz.window, c * sz.cols + hi * sz.window : c * sz.cols + (hi + 1) * sz.window]
            for hi in range(sz.high)
            for lo in range(sz.low)
        ]
        out_ref[index, c] = jnp.concatenate(pieces, axis=1)


def run(coefficients, rotation, potential, index_map, counts, box, early):
    bands, groups = lax.axis_size("band"), lax.axis_size("ga")
    sz = Sizes(box, box // 2)
    depth, _, slots = coefficients.shape
    cols = rotation.shape[2]
    panel = cols * groups
    own = panel // (bands * groups)
    consts = [jnp.asarray(t) for t in tables(sz)]
    hbm = pl.BlockSpec(memory_space=pl.ANY)
    dma = pltpu.SemaphoreType.DMA
    return pl.pallas_call(
        functools.partial(whole_kernel, bands, groups, sz, early),
        out_shape=jax.ShapeDtypeStruct((own, 2, sz.window, sz.window * sz.window), F32),
        in_specs=[hbm] * 10,
        out_specs=pl.BlockSpec(memory_space=pltpu.VMEM),
        scratch_shapes=[
            pltpu.VMEM((2, depth, slots), F32),
            pltpu.VMEM((2, cols, depth), F32),
            pltpu.VMEM((1, index_map.shape[0]), I32),
            pltpu.SMEM(counts.shape, I32),
            *[pltpu.VMEM(table.shape, table.dtype) for table in consts],
            pltpu.VMEM((2, 2 * sz.cols, 2 * sz.wide), BF16),
            pltpu.VMEM((2, 2 * sz.wide, 2 * sz.cols), BF16),
            pltpu.VMEM((sz.fold * sz.rows, index_map.shape[0]), BF16),
            pltpu.VMEM((sz.lanes, index_map.shape[0]), BF16),
            pltpu.VMEM((2, 2 * depth, slots), BF16),
            pltpu.VMEM((groups, 2, cols, depth), F32),
            pltpu.VMEM((panel, 2, slots), F32),
            pltpu.VMEM((bands * groups, own, 2, slots), F32),
            pltpu.VMEM((groups,) + potential.shape, F32),
            pltpu.VMEM((sz.fold * sz.rows, 4 * sz.lanes), F32),
            pltpu.VMEM((2 * sz.deep, sz.wide), F32),
            pltpu.VMEM((sz.rows, sz.cols), F32),
            dma((10,)),
            dma((2,)),
            dma((groups,)),
            dma((groups,)),
            dma((groups,)),
            dma((groups,)),
            dma((bands, 2)),
            dma((bands, 2)),
            dma((bands * groups,)),
            dma((bands * groups,)),
        ],
        compiler_params=pltpu.CompilerParams(
            collective_id=0, has_side_effects=True, vmem_limit_bytes=60 * 1024 * 1024
        ),
    )(coefficients, rotation.transpose(0, 2, 1), potential, index_map[None], counts, *consts)


def per_device(coefficients, rotation, potential, index_map, counts):
    groups = lax.axis_size("ga")
    return run(coefficients, rotation, potential, index_map, counts, potential.shape[0], groups // 2)


def solution(mesh):
    placed = (P("band", None, "ga"), P(None, "band", "ga"), P(None, "ga"), P(), P())
    return jax.shard_map(
        per_device,
        mesh=mesh,
        in_specs=placed,
        out_specs=P(("band", "ga"), None, None, None),
        check_vma=False,
    )
```

time: 49.4 us -> 41.1 us (0.83)
  the two profiles are of different devices: /device:TPU:0 before, /device:TPU:17 now
where the time goes in v1:
time: 41.1 us; the launch traced here: 40.9 us
  Pallas kernels  39.2 us (95%)
  local copies, waits for them, and re-layouts  1.67 us (4%)
    pallas_call x1, Pallas kernels, run(): pl.pallas_call(functools.partial(whole_kernel, bands, groups, sz, early),...  39.2 us
    unnamed x1, local copies, waits for them, and re-layouts  1.67 us

profile of v1, /device:TPU:17, one launch (start us, length us, event | category | flops | bytes accessed | tf_op | source)
XLA Modules:
  0.0 40.9 jit_solution(15196815207478308945)
XLA Ops:
  0.0 39.2 %shard_map.100 = f32[1,2,32,1024]{3,2,1,0:T(8,128)} custom-call(f32[1024,2,512]{2,1,0:T(2,128)} %coef_hbm.1, f32[2,2,1024]{2,1,0:T(2,128)} %bitcast.3, f32[64,256]{1,0:T(8,128)} %pot_hbm.1, s32[1,8192]{1,0:T(1,128)} %bitcast.2, s32[16]{0:T(128)} %cnt_hbm.1, f32[2,40,1024]{2,1,0:T(8,128)} %constant.10.clone.base_hbm, f32[2,80,256]{2,1,0:T(8,128)} %constant.11.clone.flip_hbm, ...), custom_call_target="tpu_custom_call" | custom-call | tf_op jit(solution)/shard_map/pallas_call | solution.py:413
  39.3 1.7 %copy.12 = f32[1,2,32,1024]{3,2,1,0:T(8,128)} copy(f32[1,2,32,1024]{3,2,1,0:T(8,128)} %shard_map.100) | data formatting | bytes 524288

commit v2 on v1

--- a/solution.py
+++ b/solution.py
@@ -75,7 +75,7 @@
 
 
 def whole_kernel(
-    bands, groups, sz, early, coef_hbm, rot_hbm, pot_hbm, idx_hbm, cnt_hbm, base_hbm, flip_hbm, twist_hbm,
+    bands, groups, sz, coef_hbm, rot_hbm, pot_hbm, idx_hbm, cnt_hbm, base_hbm, flip_hbm, twist_hbm,
     fore_hbm, back_hbm, out_ref, coef, rot_ref, idx, cnt, base, flip, twist, fore, back, right, right_t,
     rows_hot, cols_hot, parts, rots, prod, land, pot, grid, space, kin, load_sem, self_sem, rot_send,
     rot_recv, pot_send, pot_recv, pass_send, pass_recv, val_send, val_recv
@@ -110,68 +110,96 @@
     for item in small[:4] + coef_load + small[4:]:
         item.start()
 
+    near = 4 if groups % 4 == 0 else 1
+    lines = groups // near
+    assert groups & (groups - 1) == 0
+
+    def flip_bits(value, mask, count):
+        total, bit = 0, 1
+        while bit < count:
+            ours, theirs = lax.rem(value // bit, 2), lax.rem(mask // bit, 2) if not isinstance(mask, int) else mask // bit % 2
+            total = total + bit * (ours + theirs - 2 * ours * theirs)
+            bit *= 2
+        return total
+
+    def peer(step):
+        return flip_bits(me, step, groups)
+
     barrier = pltpu.get_barrier_semaphore()
-    peers = [(db, dg) for db in range(bands) for dg in range(groups) if db or dg]
-
-    def ahead(db, dg):
-        return {"band": lax.rem(band + db, bands), "ga": lax.rem(me + dg, groups)}
-
-    def every(act):
-        if len(peers) < 64:
-            for db, dg in peers:
-                act(db, dg)
-        else:
-
-            def body(step, carry):
-                act(step // groups, lax.rem(step, groups))
-                return carry
-
-            lax.fori_loop(1, bands * groups, body, 0)
-
-    def greet(db, dg):
-        pl.semaphore_signal(barrier, inc=1, device_id=ahead(db, dg), device_id_type=MESH)
-
-    every(greet)
+    hops = [(0, near * z) for z in range(1, lines)] + [(0, p) for p in range(1, near)]
+    hops += [(db, 0) for db in range(1, bands)]
+
+    def ahead(db, step):
+        return {"band": lax.rem(band + db, bands), "ga": peer(step)}
+
+    for db, step in hops:
+        pl.semaphore_signal(barrier, inc=1, device_id=ahead(db, step), device_id_type=MESH)
     rot_load.wait()
     rot_self = pltpu.make_async_copy(rot_hbm, rots.at[me], self_sem.at[0])
     rot_self.start()
     pot_self = pltpu.make_async_copy(pot_hbm.at[share(band)], pot.at[0, share(band)], self_sem.at[1])
     pot_self.start()
-    pl.semaphore_wait(barrier, bands * groups - 1)
-
-    def rot_copy(step):
+    pl.semaphore_wait(barrier, len(hops))
+
+    def rot_copy(z, p):
+        slot = peer(near * z) if p else me
         return pltpu.make_async_remote_copy(
-            src_ref=rot_ref, dst_ref=rots.at[me], send_sem=rot_send.at[step], recv_sem=rot_recv.at[step],
-            device_id={"band": band, "ga": lax.rem(me + step, groups)}, device_id_type=MESH,
-        )
-
-    def pot_copy(step):
+            src_ref=rots.at[slot] if z and p else rot_ref, dst_ref=rots.at[slot],
+            send_sem=rot_send.at[near * z + p], recv_sem=rot_recv.at[near * z + p],
+            device_id=ahead(0, p if p else near * z), device_id_type=MESH,
+        )
+
+    def pot_line(z):
         return pltpu.make_async_remote_copy(
-            src_ref=pot_hbm.at[share(band)], dst_ref=pot.at[step, share(band)],
-            send_sem=pot_send.at[step], recv_sem=pot_recv.at[step],
-            device_id={"band": band, "ga": lax.rem(me + step, groups)}, device_id_type=MESH,
-        )
-
-    def pass_copy(piece, db, holder):
-        held = pot.at[pl.ds(piece[0], piece[1] - piece[0]), share(holder)]
+            src_ref=pot_hbm.at[share(band)], dst_ref=pot.at[z, share(band)],
+            send_sem=pot_send.at[z], recv_sem=pot_recv.at[z],
+            device_id=ahead(0, near * z), device_id_type=MESH,
+        )
+
+    def pot_plane(p):
         return pltpu.make_async_remote_copy(
-            src_ref=held, dst_ref=held, send_sem=pass_send.at[db, piece[2]], recv_sem=pass_recv.at[db, piece[2]],
-            device_id={"band": lax.rem(band + db, bands), "ga": me}, device_id_type=MESH,
-        )
-
-    def val_copy(db, dg):
-        to = ahead(db, dg)
+            src_ref=pot.at[pl.ds(0, lines), share(band)], dst_ref=pot.at[pl.ds(p * lines, lines), share(band)],
+            send_sem=pot_send.at[lines + p], recv_sem=pot_recv.at[lines + p],
+            device_id=ahead(0, p), device_id_type=MESH,
+        )
+
+    def pass_copy(p, db, holder):
+        held = pot.at[pl.ds(p * lines, lines), share(holder)]
         return pltpu.make_async_remote_copy(
-            src_ref=prod.at[pl.ds((to["band"] * groups + to["ga"]) * own, own)], dst_ref=land.at[db * groups + dg],
-            send_sem=val_send.at[db * groups + dg], recv_sem=val_recv.at[db * groups + dg],
-            device_id=to, device_id_type=MESH,
-        )
-
-    pieces = [(0, early, 0), (early, groups, 1)]
-    for step in range(1, groups):
-        rot_copy(step).start()
-    for step in range(1, early):
-        pot_copy(step).start()
+            src_ref=held, dst_ref=held, send_sem=pass_send.at[db, p], recv_sem=pass_recv.at[db, p],
+            device_id=ahead(db, 0), device_id_type=MESH,
+        )
+
+    def val_copy(db, step):
+        to = ahead(db, step)
+        at = db * groups + step
+        return pltpu.make_async_remote_copy(
+            src_ref=prod.at[pl.ds((to["band"] * groups + to["ga"]) * own, own)], dst_ref=land.at[at],
+            send_sem=val_send.at[at], recv_sem=val_recv.at[at], device_id=to, device_id_type=MESH,
+        )
+
+    def pot_slot(ga):
+        step = peer(ga)
+        return lax.rem(step, near) * lines + step // near
+
+    def every(act):
+        if bands * groups <= 64:
+            for step in reversed(range(groups)):
+                for db in range(bands):
+                    if db or step:
+                        act(db, step)
+        else:
+
+            def body(at, carry):
+                act(at // groups, lax.rem(at, groups))
+                return carry
+
+            lax.fori_loop(1, bands * groups, body, 0)
+
+    for z in range(1, lines):
+        rot_copy(z, 0).start()
+    for p in range(1, near):
+        rot_copy(0, p).start()
 
     small[0].wait()
 
@@ -190,6 +218,8 @@
         return carry
 
     lax.fori_loop(0, sz.high, fill_right, 0)
+    for z in range(1, lines):
+        pot_line(z).start()
     small[1].wait()
 
     def fill_right_t(step, carry):
@@ -207,6 +237,10 @@
         return carry
 
     lax.fori_loop(0, sz.span, fill_right_t, 0)
+    for z in range(1, lines):
+        rot_copy(z, 0).wait_recv()
+        for p in range(1, near):
+            rot_copy(z, p).start()
     small[2].wait()
     small[3].wait()
     bits = sz.box.bit_length() - 1
@@ -253,8 +287,9 @@
         item.wait()
 
     rot_self.wait()
-    for step in range(1, groups):
-        rot_copy(step).wait_recv()
+    for z in range(lines):
+        for p in range(1, near):
+            rot_copy(z, p).wait_recv()
     real = rots[:, 0].reshape(panel, depth)
     imag = rots[:, 1].reshape(panel, depth)
     mixer = jnp.concatenate(
@@ -266,66 +301,74 @@
     prod[:, 0, :] = mixed[:panel]
     prod[:, 1, :] = mixed[panel:]
 
-    every(lambda db, dg: val_copy(db, dg).start())
-    val_self = prod.at[pl.ds(flat * own, own)]
-    for step in range(early, groups):
-        pot_copy(step).start()
-
-    def relay(piece):
-        for step in range(max(piece[0], 1), piece[1]):
-            pot_copy(step).wait_recv()
-        for db in range(1, bands):
-            pass_copy(piece, db, band).start()
-
+    every(lambda db, step: val_copy(db, step).start())
+    land[0] = prod[pl.ds(flat * own, own)]
     pot_self.wait()
-    relay(pieces[0])
-
-    batch = 4 if groups % 4 == 0 else 1
+    for z in range(1, lines):
+        pot_line(z).wait_recv()
+    for p in range(1, near):
+        pot_plane(p).start()
+    for db in range(1, bands):
+        pass_copy(0, db, band).start()
+
     for i in range(own):
-        for start in range(0, groups, batch):
+
+        def scatter(z, carry, i=i):
             total = None
-            for dg in range(start, start + batch):
-                values = val_self[i] if dg == 0 else None
+            for p in range(near):
+                step = near * z + p
+                values = None
                 for db in range(bands):
-                    if i == 0 and (db or dg):
-                        val_copy(db, dg).wait_recv()
-                    if db or dg:
-                        piece = land[db * groups + dg, i]
-                        values = piece if values is None else values + piece
-                source = lax.rem(me + groups - dg, groups)
-                at = pl.ds(pl.multiple_of(source * slots, slots), slots)
+                    if i == 0:
+                        if db or p:
+                            val_copy(db, step).wait_recv()
+                        else:
+                            pl.when(z > 0)(lambda: val_copy(0, step).wait_recv())
+                    piece = land[db * groups + step, i]
+                    values = piece if values is None else values + piece
+                at = pl.ds(pl.multiple_of(peer(step) * slots, slots), slots)
                 hits = cols_hot[:, at]
                 placed = jnp.concatenate(
                     [hits * part[c : c + 1, :] for part in split_parts(values) for c in range(2)], axis=0
                 )
                 term = dot(rows_hot[:, at], placed, ((1,), (1,)))
                 total = term if total is None else total + term
-            if start:
-                grid[...] += total
-            else:
-                grid[...] = total
+            grid[...] += total
+            return carry
+
+        grid[...] = jnp.zeros_like(grid)
+        lax.fori_loop(0, lines, scatter, 0)
         if i == 0:
-            relay(pieces[1])
+            for p in range(1, near):
+                pot_plane(p).wait_recv()
+                for db in range(1, bands):
+                    pass_copy(p, db, band).start()
 
         def pot_ready():
-            for piece in pieces:
+            for p in range(near):
                 for db in range(1, bands):
-                    pass_copy(piece, db, lax.rem(band + bands - db, bands)).wait_recv()
+                    pass_copy(p, db, lax.rem(band + bands - db, bands)).wait_recv()
 
         apply_kernel(
-            groups, sz, i, me, pot_ready if i == 0 else None, grid, pot, right, right_t, fore, back, twist, kin, space, out_ref
-        )
-    every(lambda db, dg: val_copy(db, dg).wait_send())
-    for step in range(1, groups):
-        rot_copy(step).wait_send()
-        pot_copy(step).wait_send()
-    for piece in pieces:
+            sz, i, pot_ready if i == 0 else None, grid, lambda ga: pot[pot_slot(ga)], pot.shape[2], groups, right,
+            right_t, fore, back, twist, kin, space, out_ref
+        )
+    every(lambda db, step: val_copy(db, step).wait_send())
+    for z in range(lines):
+        for p in range(near):
+            if z or p:
+                rot_copy(z, p).wait_send()
+    for z in range(1, lines):
+        pot_line(z).wait_send()
+    for p in range(1, near):
+        pot_plane(p).wait_send()
+    for p in range(near):
         for db in range(1, bands):
-            pass_copy(piece, db, band).wait_send()
+            pass_copy(p, db, band).wait_send()
 
 
 def apply_kernel(
-    groups, sz, index, me, pot_ready, grid, pot, right, right_t, fore, back, twist, kin, space, out_ref
+    sz, index, pot_ready, grid, pot_block, each, groups, right, right_t, fore, back, twist, kin, space, out_ref
 ):
     whole = 2 * sz.lanes
     summed = grid[:, :whole] + grid[:, whole:]
@@ -362,7 +405,6 @@
         space[:, at : at + step] = dot(fore[0], high) + (dot(fore[0], low) + dot(fore[1], high))
     if pot_ready is not None:
         pot_ready()
-    each = pot.shape[2]
     per = groups // sz.low
     applied = None
     for at in range(0, sz.wide, step):
@@ -370,7 +412,7 @@
         for k_high in range(sz.low):
             lane = []
             for q in range(at // each, (at + step + each - 1) // each):
-                lane.append(pot[lax.rem(me + groups - (k_high * per + q), groups)])
+                lane.append(pot_block(k_high * per + q))
             blocks.append(lane[0] if len(lane) == 1 else jnp.concatenate(lane, axis=1))
         local = jnp.concatenate(blocks, axis=0)
         high, low = split_parts(space[:, at : at + step] * jnp.concatenate([local, local], axis=0))
@@ -400,7 +442,7 @@
         out_ref[index, c] = jnp.concatenate(pieces, axis=1)
 
 
-def run(coefficients, rotation, potential, index_map, counts, box, early):
+def run(coefficients, rotation, potential, index_map, counts, box):
     bands, groups = lax.axis_size("band"), lax.axis_size("ga")
     sz = Sizes(box, box // 2)
     depth, _, slots = coefficients.shape
@@ -411,7 +453,7 @@
     hbm = pl.BlockSpec(memory_space=pl.ANY)
     dma = pltpu.SemaphoreType.DMA
     return pl.pallas_call(
-        functools.partial(whole_kernel, bands, groups, sz, early),
+        functools.partial(whole_kernel, bands, groups, sz),
         out_shape=jax.ShapeDtypeStruct((own, 2, sz.window, sz.window * sz.window), F32),
         in_specs=[hbm] * 10,
         out_specs=pl.BlockSpec(memory_space=pltpu.VMEM),
@@ -439,8 +481,8 @@
             dma((groups,)),
             dma((groups,)),
             dma((groups,)),
-            dma((bands, 2)),
-            dma((bands, 2)),
+            dma((bands, 4)),
+            dma((bands, 4)),
             dma((bands * groups,)),
             dma((bands * groups,)),
         ],
@@ -451,8 +493,7 @@
 
 
 def per_device(coefficients, rotation, potential, index_map, counts):
-    groups = lax.axis_size("ga")
-    return run(coefficients, rotation, potential, index_map, counts, potential.shape[0], groups // 2)
+    return run(coefficients, rotation, potential, index_map, counts, potential.shape[0])
 
 
 def solution(mesh):

time: 41.1 us -> 31.3 us (0.76)
  the two profiles are of different devices: /device:TPU:17 before, /device:TPU:0 now
where the time goes in v2:
time: 31.3 us; the launch traced here: 31.1 us
  Pallas kernels  29.4 us (94%)
  local copies, waits for them, and re-layouts  1.67 us (5%)
    pallas_call x1, Pallas kernels, run(): pl.pallas_call(functools.partial(whole_kernel, bands, groups, sz), out_sh...  29.4 us
    unnamed x1, local copies, waits for them, and re-layouts  1.67 us

profile of v2, /device:TPU:0, one launch (start us, length us, event | category | flops | bytes accessed | tf_op | source)
XLA Modules:
  0.0 31.1 jit_solution(9705621612887611107)
XLA Ops:
  0.0 29.4 %shard_map.100 = f32[1,2,32,1024]{3,2,1,0:T(8,128)} custom-call(f32[1024,2,512]{2,1,0:T(2,128)} %coef_hbm.1, f32[2,2,1024]{2,1,0:T(2,128)} %bitcast.3, f32[64,256]{1,0:T(8,128)} %pot_hbm.1, s32[1,8192]{1,0:T(1,128)} %bitcast.2, s32[16]{0:T(128)} %cnt_hbm.1, f32[2,40,1024]{2,1,0:T(8,128)} %constant.10.clone.base_hbm, f32[2,80,256]{2,1,0:T(8,128)} %constant.11.clone.flip_hbm, ...), custom_call_target="tpu_custom_call" | custom-call | tf_op jit(solution)/shard_map/pallas_call | solution.py:455
  29.4 1.7 %copy.12 = f32[1,2,32,1024]{3,2,1,0:T(8,128)} copy(f32[1,2,32,1024]{3,2,1,0:T(8,128)} %shard_map.100) | data formatting | bytes 524288

commit v3 on v2

--- a/solution.py
+++ b/solution.py
@@ -454,7 +454,7 @@
     dma = pltpu.SemaphoreType.DMA
     return pl.pallas_call(
         functools.partial(whole_kernel, bands, groups, sz),
-        out_shape=jax.ShapeDtypeStruct((own, 2, sz.window, sz.window * sz.window), F32),
+        out_shape=pltpu.VMEM((own, 2, sz.window, sz.window * sz.window), F32),
         in_specs=[hbm] * 10,
         out_specs=pl.BlockSpec(memory_space=pltpu.VMEM),
         scratch_shapes=[

time: 31.3 us -> 29.7 us (0.949)
  local copies, waits for them, and re-layouts: 1.67 us -> 0.71 us
  Pallas kernels: 29.4 us -> 28.7 us
    unnamed x1, local copies, waits for them, and re-layouts: 1.67 us -> 0.71 us
    pallas_call x1, Pallas kernels: 29.4 us -> 28.7 us  [run(): pl.pallas_call(functools.partial(whole_kernel, bands, groups, sz), out_sh...]
where the time goes in v3:
time: 29.7 us; the launch traced here: 29.4 us
  Pallas kernels  28.7 us (97%)
  local copies, waits for them, and re-layouts  0.71 us (2%)
    pallas_call x1, Pallas kernels, run(): pl.pallas_call(functools.partial(whole_kernel, bands, groups, sz), out_sh...  28.7 us
    unnamed x1, local copies, waits for them, and re-layouts  0.71 us

profile of v3, /device:TPU:0, one launch (start us, length us, event | category | flops | bytes accessed | tf_op | source)
XLA Modules:
  0.0 29.4 jit_solution(3561259388320069139)
XLA Ops:
  0.0 28.7 %shard_map.100 = f32[1,2,32,1024]{3,2,1,0:T(8,128)S(1)} custom-call(f32[1024,2,512]{2,1,0:T(2,128)} %coef_hbm.1, f32[2,2,1024]{2,1,0:T(2,128)} %bitcast.3, f32[64,256]{1,0:T(8,128)} %pot_hbm.1, s32[1,8192]{1,0:T(1,128)} %bitcast.2, s32[16]{0:T(128)} %cnt_hbm.1, f32[2,40,1024]{2,1,0:T(8,128)} %constant.10.clone.base_hbm, ...), custom_call_target="tpu_custom_call" | custom-call | tf_op jit(solution)/shard_map/pallas_call | solution.py:455
  28.7 0.7 %copy.12 = f32[1,2,32,1024]{3,2,1,0:T(8,128)} copy(f32[1,2,32,1024]{3,2,1,0:T(8,128)S(1)} %shard_map.100) | data formatting | bytes 524288

commit v4 on v3

--- a/solution.py
+++ b/solution.py
@@ -61,12 +61,14 @@
         [pair(np.tile(z_phase.T, (1, sz.high))), pair(np.repeat(y_phase.T, sz.window, axis=1))], axis=1
     )
     twist = pair(np.repeat(digit[:, None] * k_low[None, :], sz.box, axis=1))
-    l_phase = sz.span * digit[:, None] * digit[None, :]
-    x_phase = k_all[:, None] * n_signed[None, :]
-    left = (l_phase[:, None, :, None] + x_phase[None, :, None, :]).reshape(sz.deep, sz.rows)
-    cos, sin = pair(left)
-    fore = two_parts((np.block([[cos, -sin], [sin, cos]]) / sz.box**3).astype(np.float32))
-    back = two_parts(np.block([[cos.T, sin.T], [-sin.T, cos.T]]).astype(np.float32))
+    cos, sin = pair(k_all[:, None] * n_signed[None, :])
+
+    def three(table):
+        high, low = two_parts(table.astype(np.float32))
+        return np.concatenate([high, high, low], axis=1)
+
+    fore = three(np.block([[cos, -sin], [sin, cos]]) / sz.box**3)
+    back = three(np.block([[cos.T, sin.T], [-sin.T, cos.T]]))
     return base.astype(np.float32), flip.astype(np.float32), twist.astype(np.float32), fore, back
 
 
@@ -310,6 +312,12 @@
         pot_plane(p).start()
     for db in range(1, bands):
         pass_copy(0, db, band).start()
+
+    def relay(pieces):
+        for p in pieces:
+            pot_plane(p).wait_recv()
+            for db in range(1, bands):
+                pass_copy(p, db, band).start()
 
     for i in range(own):
 
@@ -339,10 +347,7 @@
         grid[...] = jnp.zeros_like(grid)
         lax.fori_loop(0, lines, scatter, 0)
         if i == 0:
-            for p in range(1, near):
-                pot_plane(p).wait_recv()
-                for db in range(1, bands):
-                    pass_copy(p, db, band).start()
+            relay(range(1, near))
 
         def pot_ready():
             for p in range(near):
@@ -365,6 +370,19 @@
     for p in range(near):
         for db in range(1, bands):
             pass_copy(p, db, band).wait_send()
+
+
+def quarter(real, imag, sign):
+    even_r, even_i = real[0] + real[2], imag[0] + imag[2]
+    odd_r, odd_i = real[0] - real[2], imag[0] - imag[2]
+    both_r, both_i = real[1] + real[3], imag[1] + imag[3]
+    gap_r, gap_i = sign * (real[1] - real[3]), sign * (imag[1] - imag[3])
+    return (
+        (even_r + both_r, even_i + both_i),
+        (odd_r - gap_i, odd_i + gap_r),
+        (even_r - both_r, even_i - both_i),
+        (odd_r + gap_i, odd_i - gap_r),
+    )
 
 
 def apply_kernel(
@@ -390,41 +408,36 @@
                 dot(field_high, right[0, :, here])
                 + (dot(field_low, right[0, :, here]) + dot(field_high, right[1, :, here]))
             )
-        real = halves[0].reshape(sz.low, sz.window, step)
-        imag = halves[1].reshape(sz.low, sz.window, step)
-        cos = twist[0, :, at : at + step][:, None, :]
-        sin = twist[1, :, at : at + step][:, None, :]
-        turned = jnp.concatenate(
-            [
-                (real * cos - imag * sin).reshape(sz.rows, step),
-                (real * sin + imag * cos).reshape(sz.rows, step),
-            ],
-            axis=0,
-        )
-        high, low = split_parts(turned)
-        space[:, at : at + step] = dot(fore[0], high) + (dot(fore[0], low) + dot(fore[1], high))
+        real, imag = [], []
+        for l in range(sz.low):
+            cos, sin = twist[0, l : l + 1, at : at + step], twist[1, l : l + 1, at : at + step]
+            a, b = [half[l * sz.window : (l + 1) * sz.window] for half in halves]
+            real.append(a * cos - b * sin)
+            imag.append(a * sin + b * cos)
+        for k, (a, b) in enumerate(quarter(real, imag, 1)):
+            high, low = split_parts(jnp.concatenate([a, b], axis=0))
+            stacked = jnp.concatenate([high, low, high], axis=0)
+            space[k * 2 * sz.box : (k + 1) * 2 * sz.box, at : at + step] = dot(fore[...], stacked)
     if pot_ready is not None:
         pot_ready()
     per = groups // sz.low
     applied = None
     for at in range(0, sz.wide, step):
-        blocks = []
-        for k_high in range(sz.low):
-            lane = []
-            for q in range(at // each, (at + step + each - 1) // each):
-                lane.append(pot_block(k_high * per + q))
-            blocks.append(lane[0] if len(lane) == 1 else jnp.concatenate(lane, axis=1))
-        local = jnp.concatenate(blocks, axis=0)
-        high, low = split_parts(space[:, at : at + step] * jnp.concatenate([local, local], axis=0))
-        spread = dot(back[0], high) + (dot(back[0], low) + dot(back[1], high))
-        real = spread[: sz.rows].reshape(sz.low, sz.window, step)
-        imag = spread[sz.rows :].reshape(sz.low, sz.window, step)
-        cos = twist[0, :, at : at + step][:, None, :]
-        sin = twist[1, :, at : at + step][:, None, :]
-        turned = [
-            (real * cos + imag * sin).reshape(sz.rows, step),
-            (imag * cos - real * sin).reshape(sz.rows, step),
-        ]
+        real, imag = [], []
+        for k in range(sz.low):
+            lane = [pot_block(k * per + q) for q in range(at // each, (at + step + each - 1) // each)]
+            local = lane[0] if len(lane) == 1 else jnp.concatenate(lane, axis=1)
+            here = space[k * 2 * sz.box : (k + 1) * 2 * sz.box, at : at + step]
+            high, low = split_parts(here * jnp.concatenate([local, local], axis=0))
+            spread = dot(back[...], jnp.concatenate([high, low, high], axis=0))
+            real.append(spread[: sz.window])
+            imag.append(spread[sz.window :])
+        turned = [[], []]
+        for l, (a, b) in enumerate(quarter(real, imag, -1)):
+            cos, sin = twist[0, l : l + 1, at : at + step], twist[1, l : l + 1, at : at + step]
+            turned[0].append(a * cos + b * sin)
+            turned[1].append(b * cos - a * sin)
+        turned = [jnp.concatenate(rows, axis=0) for rows in turned]
         for c in range(2):
             here = slice(c * sz.wide + at, c * sz.wide + at + step)
             high, low = split_parts(turned[c])

time: 29.7 us -> 28.2 us (0.949)
  Pallas kernels: 28.7 us -> 27.2 us
    pallas_call x1, Pallas kernels: 28.7 us -> 27.2 us  [run(): pl.pallas_call(functools.partial(whole_kernel, bands, groups, sz), out_sh...]
where the time goes in v4:
time: 28.2 us; the launch traced here: 27.9 us
  Pallas kernels  27.2 us (96%)
  local copies, waits for them, and re-layouts  0.71 us (3%)
    pallas_call x1, Pallas kernels, run(): pl.pallas_call(functools.partial(whole_kernel, bands, groups, sz), out_sh...  27.2 us
    unnamed x1, local copies, waits for them, and re-layouts  0.71 us

profile of v4, /device:TPU:0, one launch (start us, length us, event | category | flops | bytes accessed | tf_op | source)
XLA Modules:
  0.0 27.9 jit_solution(14143899143248181903)
XLA Ops:
  0.0 27.2 %shard_map.100 = f32[1,2,32,1024]{3,2,1,0:T(8,128)S(1)} custom-call(f32[1024,2,512]{2,1,0:T(2,128)} %coef_hbm.1, f32[2,2,1024]{2,1,0:T(2,128)} %bitcast.3, f32[64,256]{1,0:T(8,128)} %pot_hbm.1, s32[1,8192]{1,0:T(1,128)} %bitcast.2, s32[16]{0:T(128)} %cnt_hbm.1, f32[2,40,1024]{2,1,0:T(8,128)} %constant.10.clone.base_hbm, ...), custom_call_target="tpu_custom_call" | custom-call | tf_op jit(solution)/shard_map/pallas_call | solution.py:468
  27.2 0.7 %copy.12 = f32[1,2,32,1024]{3,2,1,0:T(8,128)} copy(f32[1,2,32,1024]{3,2,1,0:T(8,128)S(1)} %shard_map.100) | data formatting | bytes 524288

commit v5 on v4

--- a/solution.py
+++ b/solution.py
@@ -220,8 +220,6 @@
         return carry
 
     lax.fori_loop(0, sz.high, fill_right, 0)
-    for z in range(1, lines):
-        pot_line(z).start()
     small[1].wait()
 
     def fill_right_t(step, carry):
@@ -243,6 +241,8 @@
         rot_copy(z, 0).wait_recv()
         for p in range(1, near):
             rot_copy(z, p).start()
+    for z in range(1, lines):
+        pot_line(z).start()
     small[2].wait()
     small[3].wait()
     bits = sz.box.bit_length() - 1
@@ -308,7 +308,7 @@
     pot_self.wait()
     for z in range(1, lines):
         pot_line(z).wait_recv()
-    for p in range(1, near):
+    for p in reversed(range(1, near)):
         pot_plane(p).start()
     for db in range(1, bands):
         pass_copy(0, db, band).start()
@@ -350,6 +350,15 @@
             relay(range(1, near))
 
         def pot_ready():
+            every(lambda db, step: val_copy(db, step).wait_send())
+            for z in range(lines):
+                for p in range(near):
+                    if z or p:
+                        rot_copy(z, p).wait_send()
+            for z in range(1, lines):
+                pot_line(z).wait_send()
+            for p in range(1, near):
+                pot_plane(p).wait_send()
             for p in range(near):
                 for db in range(1, bands):
                     pass_copy(p, db, lax.rem(band + bands - db, bands)).wait_recv()
@@ -358,15 +367,6 @@
             sz, i, pot_ready if i == 0 else None, grid, lambda ga: pot[pot_slot(ga)], pot.shape[2], groups, right,
             right_t, fore, back, twist, kin, space, out_ref
         )
-    every(lambda db, step: val_copy(db, step).wait_send())
-    for z in range(lines):
-        for p in range(near):
-            if z or p:
-                rot_copy(z, p).wait_send()
-    for z in range(1, lines):
-        pot_line(z).wait_send()
-    for p in range(1, near):
-        pot_plane(p).wait_send()
     for p in range(near):
         for db in range(1, bands):
             pass_copy(p, db, band).wait_send()

time: 28.2 us -> 27.7 us (0.982)
  Pallas kernels: 27.2 us -> 26.8 us
    pallas_call x1, Pallas kernels: 27.2 us -> 26.8 us  [run(): pl.pallas_call(functools.partial(whole_kernel, bands, groups, sz), out_sh...]
where the time goes in v5:
time: 27.7 us; the launch traced here: 27.5 us
  Pallas kernels  26.8 us (97%)
  local copies, waits for them, and re-layouts  0.71 us (3%)
    pallas_call x1, Pallas kernels, run(): pl.pallas_call(functools.partial(whole_kernel, bands, groups, sz), out_sh...  26.8 us
    unnamed x1, local copies, waits for them, and re-layouts  0.71 us

profile of v5, /device:TPU:0, one launch (start us, length us, event | category | flops | bytes accessed | tf_op | source)
XLA Modules:
  0.0 27.5 jit_solution(14575332049064537575)
XLA Ops:
  0.0 26.8 %shard_map.100 = f32[1,2,32,1024]{3,2,1,0:T(8,128)S(1)} custom-call(f32[1024,2,512]{2,1,0:T(2,128)} %coef_hbm.1, f32[2,2,1024]{2,1,0:T(2,128)} %bitcast.3, f32[64,256]{1,0:T(8,128)} %pot_hbm.1, s32[1,8192]{1,0:T(1,128)} %bitcast.2, s32[16]{0:T(128)} %cnt_hbm.1, f32[2,40,1024]{2,1,0:T(8,128)} %constant.10.clone.base_hbm, ...), custom_call_target="tpu_custom_call" | custom-call | tf_op jit(solution)/shard_map/pallas_call | solution.py:468
  26.8 0.7 %copy.12 = f32[1,2,32,1024]{3,2,1,0:T(8,128)} copy(f32[1,2,32,1024]{3,2,1,0:T(8,128)S(1)} %shard_map.100) | data formatting | bytes 524288
